TPU v7x, 512 devices: a whole 4x8x8 slice. The times are simulated.
512 devices in a mesh: gx: 8 (over z), gy: 4 (over x), gz: 16 (over y, core).
Axes of the slice: x: 4, y: 8, z: 8, core: 2. Of those that a mesh axis runs over, the one named last changes fastest.
Arguments:
- acts: bfloat16 [655360, 768], P(('gx', 'gy', 'gz')), may hold values from -24 to 24
- grads_out: bfloat16 [655360, 768], P(('gx', 'gy', 'gz')), may hold values from -0.0078125 to 0.0078125
- master: float32 [4608, 128], P(('gx', 'gy', 'gz')), may hold values from -0.3 to 0.3
- moment: float32 [4608, 128], P(('gx', 'gy', 'gz')), may hold values from -6 to 6
- second: float32 [4608, 128], P(('gx', 'gy', 'gz')), may hold values from 0.1 to 2
Outputs:
- master_new: float32 [4608, 128], P(('gx', 'gy', 'gz'))
- moment_new: float32 [4608, 128], P(('gx', 'gy', 'gz'))
- second_new: float32 [4608, 128], P(('gx', 'gy', 'gz'))
- weights: bfloat16 [768, 768], replicated
All inputs are finite; a program needn't handle non-finite values.
Results may differ from a plain program's by a relative error of at most 0.003.
Values may be sent and summed in bfloat16 or wider, within the bound.
A program may use at most 64 MiB of HBM per device.

v0:
```python
import jax
import jax.numpy as jnp
from jax import lax
from jax.sharding import PartitionSpec as P

STEP = 1000


def in_blocks(x, dim, length):
    shape = x.shape
    parts = x.reshape(*shape[:dim], length, shape[dim] // length, *shape[dim + 1 :])
    return jnp.moveaxis(parts, dim, 0)


def sent_and_summed(x, axis, dim):
    parts = in_blocks(x, dim, lax.axis_size(axis))
    arrived = lax.all_to_all(parts, axis, split_axis=0, concat_axis=0, tiled=True)
    return arrived.astype(jnp.float32).sum(axis=0)


def in_order(parts, dim):
    shape = list(parts.shape[1:])
    shape[dim] *= parts.shape[0]
    return jnp.moveaxis(parts, 0, dim).reshape(shape)


def sent_to_all(x, axis):
    length = lax.axis_size(axis)
    return lax.all_to_all(jnp.broadcast_to(x[None], (length, *x.shape)), axis, 0, 0, tiled=True)


def gathered_copies(x, axis, dim):
    return in_order(sent_to_all(x, axis), dim)


def shards(acts, grads_out, master, moment, second):
    width_in = acts.shape[1]
    width_out = grads_out.shape[1]
    lane = master.shape[1]
    total_rows = width_in * width_out // lane
    local_grad = lax.dot_general(
        acts, grads_out, (((0,), (0,)), ((), ())), preferred_element_type=jnp.float32
    )
    local_flat = local_grad.reshape(total_rows, lane)
    partial_value = sent_and_summed(local_flat.astype(jnp.bfloat16), "gx", 0)
    partial_value = sent_and_summed(partial_value.astype(jnp.bfloat16), "gy", 0)
    gradient = sent_and_summed(partial_value.astype(jnp.bfloat16), "gz", 0)
    moment_new = 0.9 * moment + 0.1 * gradient
    second_new = 0.95 * second + 0.05 * gradient * gradient
    first_fix = 1.0 - 0.9**STEP
    second_fix = 1.0 - 0.95**STEP
    ratio = moment_new / first_fix / (jnp.sqrt(second_new / second_fix) + 1e-08)
    master_new = master - 0.01 * (ratio + 0.01 * master)
    rounded = master_new.astype(jnp.bfloat16)
    gathered = gathered_copies(rounded, "gz", 0)
    gathered = gathered_copies(gathered, "gy", 0)
    gathered = gathered_copies(gathered, "gx", 0)
    weights = gathered.reshape(width_in, width_out)
    return (master_new, moment_new, second_new, weights)


def solution(mesh):
    return jax.shard_map(
        shards,
        mesh=mesh,
        in_specs=(
            P(("gx", "gy", "gz"), None),
            P(("gx", "gy", "gz"), None),
            P(("gx", "gy", "gz"), None),
            P(("gx", "gy", "gz"), None),
            P(("gx", "gy", "gz"), None),
        ),
        out_specs=(
            P(("gx", "gy", "gz"), None),
            P(("gx", "gy", "gz"), None),
            P(("gx", "gy", "gz"), None),
            P(),
        ),
        check_vma=False,
    )
```

profile of v0, /device:TPU:1, one launch (start us, length us, event | category | flops | bytes accessed | tf_op | source)
XLA Modules:
  0.0 132.2 jit_solution(5655682131265207856)
XLA Ops:
  0.6 0.0 copy-start
  0.6 1.5 %copy-done = bf16[1280,768]{1,0:T(8,128)(2,1)S(1)} copy-done((bf16[1280,768]{1,0:T(8,128)(2,1)S(1)}, bf16[1280,768]{1,0:T(8,128)(2,1)}, u32[]{:S(2)}) %copy-start) | copy-done | bytes 1966104
  2.2 4.3 %convolution_convert_fusion = bf16[768,768]{1,0:T(8,128)(2,1)} fusion(bf16[1280,768]{1,0:T(8,128)(2,1)S(1)} %copy-done, bf16[1280,768]{1,0:T(8,128)(2,1)} %param.6), kind=kOutput, calls=%fused_computation | convolution fusion | flops 1510539264 | bytes 5111808 | tf_op jit(solution)/shard_map/dot_general | solution.py:41
  6.5 2.6 %convert_element_type.18 = bf16[8,576,128]{2,1,0:T(8,128)(2,1)S(1)} reshape(bf16[768,768]{1,0:T(8,128)(2,1)} %convolution_convert_fusion) | data formatting | bytes 2359296 | tf_op jit(solution)/shard_map/convert_element_type | solution.py:45
  9.1 0.0 copy-start.1
  9.1 0.0 copy-start.2
  9.1 0.0 copy-start.3
  9.1 41.3 %all_to_all.30 = bf16[8,576,128]{2,1,0:T(8,128)(2,1)} all-to-all(bf16[8,576,128]{2,1,0:T(8,128)(2,1)S(1)} %convert_element_type.18), channel_id=1, replica_groups=mesh['gx'=8,'gy'=4,'gz'=16] {'gx'}, dimensions={0} | all-to-all | bytes 2359296 | tf_op jit(solution)/shard_map/all_to_all | solution.py:17
  50.4 1.4 %reduce_sum.33 = bf16[576,128]{1,0:T(8,128)(2,1)S(1)} reduce(bf16[8,576,128]{2,1,0:T(8,128)(2,1)} %all_to_all.30, bf16[]{:T(256)} %constant.3.clone.1), dimensions={0}, to_apply=%region_0.0 | reduce | flops 516096 | bytes 1327106 | tf_op jit(solution)/shard_map/reduce_sum | solution.py:18
  51.9 8.7 %all_to_all.31 = bf16[4,144,128]{2,1,0:T(8,128)(2,1)S(1)} all-to-all(bf16[4,144,128]{2,1,0:T(8,128)(2,1)S(1)} %bitcast.4), channel_id=1, replica_groups=mesh['gx'=8,'gy'=4,'gz'=16] {'gy'}, dimensions={0} | all-to-all | bytes 294912 | tf_op jit(solution)/shard_map/all_to_all | solution.py:17
  60.7 18.2 %all_to_all.32 = bf16[16,9,128]{2,1,0:T(8,128)(2,1)S(1)} all-to-all(bf16[16,9,128]{2,1,0:T(8,128)(2,1)S(1)} %reshape.22), channel_id=1, replica_groups=mesh['gx'=8,'gy'=4,'gz'=16] {'gz'}, dimensions={0} | all-to-all | bytes 73728 | tf_op jit(solution)/shard_map/all_to_all | solution.py:17
  78.8 0.0 copy-done.1
  78.9 0.0 copy-done.2
  78.9 0.0 copy-done.3
  78.9 0.6 fusion.1
  79.5 10.3 %all_to_all.33 = bf16[16,9,128]{2,1,0:T(8,128)(2,1)S(1)} all-to-all(bf16[16,9,128]{2,1,0:T(8,128)(2,1)S(1)} %broadcast_in_dim.20), channel_id=1, replica_groups=mesh['gx'=8,'gy'=4,'gz'=16] {'gz'}, dimensions={0} | all-to-all | bytes 73728 | tf_op jit(solution)/shard_map/all_to_all | solution.py:29
  89.9 7.4 %all_to_all.34 = bf16[4,144,128]{2,1,0:T(8,128)(2,1)S(1)} all-to-all(bf16[4,144,128]{2,1,0:T(8,128)(2,1)S(1)} %broadcast_in_dim.22), channel_id=1, replica_groups=mesh['gx'=8,'gy'=4,'gz'=16] {'gy'}, dimensions={0} | all-to-all | bytes 294912 | tf_op jit(solution)/shard_map/all_to_all | solution.py:29
  97.4 0.2 broadcast_in_dim.24
  97.5 32.8 %all_to_all.35 = bf16[8,576,128]{2,1,0:T(8,128)(2,1)S(1)} all-to-all(bf16[8,576,128]{2,1,0:T(8,128)(2,1)S(1)} %broadcast_in_dim.24), channel_id=1, replica_groups=mesh['gx'=8,'gy'=4,'gz'=16] {'gx'}, dimensions={0} | all-to-all | bytes 2359296 | tf_op jit(solution)/shard_map/all_to_all | solution.py:29
  130.3 1.9 %reshape_reshape.3 = bf16[768,768]{1,0:T(8,128)(2,1)} reshape(bf16[8,576,128]{2,1,0:T(8,128)(2,1)S(1)} %all_to_all.35) | data formatting | bytes 2359296 | tf_op jit(solution)/shard_map/reshape;reshape | solution.py:58
  (6 shorter events, 0.1 us)
Async XLA Ops:
  0.6 1.6 %copy-start = (bf16[1280,768]{1,0:T(8,128)(2,1)S(1)}, bf16[1280,768]{1,0:T(8,128)(2,1)}, u32[]{:S(2)}) copy-start(bf16[1280,768]{1,0:T(8,128)(2,1)} %param.5) | copy-start | bytes 5898244
  9.1 69.8 %copy-start.1 = (f32[9,128]{1,0:T(8,128)S(1)}, f32[9,128]{1,0:T(8,128)}, u32[]{:S(2)}) copy-start(f32[9,128]{1,0:T(8,128)} %param.7) | copy-start | bytes 13828
  9.1 69.8 %copy-start.2 = (f32[9,128]{1,0:T(8,128)S(1)}, f32[9,128]{1,0:T(8,128)}, u32[]{:S(2)}) copy-start(f32[9,128]{1,0:T(8,128)} %param.9) | copy-start | bytes 13828
  9.1 69.8 %copy-start.3 = (f32[9,128]{1,0:T(8,128)S(1)}, f32[9,128]{1,0:T(8,128)}, u32[]{:S(2)}) copy-start(f32[9,128]{1,0:T(8,128)} %param.8) | copy-start | bytes 13828
where the time goes:
time: 133 us; the launch traced here: 132 us
  blocking collectives  119 us (89%)
  local copies, waits for them, and re-layouts  6.21 us (5%)
  matrix products  4.3 us (3%)
  other arithmetic  2.12 us (2%)
    all_to_all x3, blocking collectives, sent_and_summed(): lax.all_to_all(parts, axis, split_axis=0, concat_axis=0, tiled=True)  68.2 us
    all_to_all x3, blocking collectives, sent_to_all(): lax.all_to_all(jnp.broadcast_to(x[None], (length, *x.shape)), axis, 0, 0,...  50.6 us
    dot_general x1, matrix products, shards(): lax.dot_general(acts, grads_out, (((0,), (0,)), ((), ())), preferred_elem...  4.3 us

commit v1 on v0

v1 whole, which is shorter than its diff:
```python
import functools

import jax
import jax.numpy as jnp
from jax import lax
from jax.experimental import pallas as pl
from jax.experimental.pallas import tpu as pltpu
from jax.sharding import PartitionSpec as P

STEP = 1000
MESH = pl.DeviceIdType.MESH
LANE = 128
NX, NY, NZ = 4, 8, 8
ROWS = 24
HALF = 384
AW = 256
CW = 128
F32 = jnp.float32
BF16 = jnp.bfloat16

D0, A1, C1, A2, C2, SS, SO = 0, 2, 5, 12, 19, 22, 29
WS, WO, GA1, GA2, GC1, GC2, DD = 37, 44, 52, 59, 62, 65, 72
NSEM = 84


def kernel(acts, grads, master, moment, second,
           master_out, moment_out, second_out, out,
           acts_v, grads_v, prod, snd0, rcv0, s_a1, r_a1, s_c1, r_c1, s_a2, r_a2, s_c2, r_c2,
           sum3, pack_s, pack_o, s_s, s_o, r_s, r_o, flat, w3s, w3o, s_wo, w24,
           send, recv, local):
    z = lax.axis_index("gx")
    x = lax.axis_index("gy")
    yc = lax.axis_index("gz")
    y = yc // 2
    core = lax.rem(yc, 2)
    other = 1 - core

    def dev(dz=0, dx=0, dy=0, flip=False):
        cc = other if flip else core
        return (lax.rem(z + dz, NZ), lax.rem(x + dx, NX), lax.rem(y + dy, NY) * 2 + cc)

    sends = []

    def push(src, dst, slot, to):
        copy = pltpu.make_async_remote_copy(
            src_ref=src, dst_ref=dst, send_sem=send.at[slot], recv_sem=recv.at[slot],
            device_id=to, device_id_type=MESH)
        copy.start()
        sends.append(copy)
        return copy

    loads = [
        pltpu.make_async_copy(acts.at[:, pl.ds(0, HALF)], acts_v.at[:, pl.ds(0, HALF)], local.at[0]),
        pltpu.make_async_copy(grads, grads_v, local.at[1]),
        pltpu.make_async_copy(acts.at[:, pl.ds(HALF, HALF)], acts_v.at[:, pl.ds(HALF, HALF)], local.at[2]),
    ]
    for load in loads:
        load.start()

    barrier = pltpu.get_barrier_semaphore()
    partners = [dev(flip=True)]
    partners += [dev(dx=k) for k in range(1, NX)]
    partners += [dev(dz=k) for k in range(1, NZ)]
    partners += [dev(dy=k) for k in range(1, NY)]
    partners += [dev(dy=k, flip=True) for k in range(1, NY)]
    for to in partners:
        pl.semaphore_signal(barrier, inc=1, device_id=to, device_id_type=MESH)

    mine = pl.ds(pl.multiple_of(core * HALF, LANE), HALF)
    theirs = pl.ds(pl.multiple_of(other * HALF, LANE), HALF)

    def multiply(m):
        prod[pl.ds(m * HALF, HALF), :] = lax.dot_general(
            acts_v[:, pl.ds(m * HALF, HALF)], grads_v[...], (((0,), (0,)), ((), ())),
            preferred_element_type=F32)
        snd0[pl.ds(16 * m, 16)] = prod[pl.ds(m * HALF, HALF), theirs].astype(BF16).reshape(16, ROWS, HALF)

    loads[0].wait()
    loads[1].wait()
    multiply(0)
    pl.semaphore_wait(barrier, len(partners))
    d0 = [push(snd0.at[pl.ds(0, 16)], rcv0.at[pl.ds(0, 16)], D0, dev(flip=True))]
    loads[2].wait()
    multiply(1)
    d0.append(push(snd0.at[pl.ds(16, 16)], rcv0.at[pl.ds(16, 16)], D0 + 1, dev(flip=True)))

    for m in range(2):
        d0[m].wait_recv()

        def add(i, carry):
            row = pl.ds(pl.multiple_of(i * ROWS, 8), ROWS)
            total = (prod[row, mine] + rcv0[i].astype(F32)).astype(BF16)
            s_a1[lax.rem(i, NX), i // NX] = total[:, :AW]
            s_c1[i // NX, lax.rem(i, NX)] = total[:, AW:]
            return carry

        lax.fori_loop(16 * m, 16 * m + 16, add, 0)

    a1 = [push(s_a1.at[lax.rem(x + k, NX)], r_a1.at[k - 1], A1 + k - 1, dev(dx=k)) for k in (2, 1, 3)]
    c1 = [push(s_c1.at[lax.rem(z + k, NZ)], r_c1.at[k - 1], C1 + k - 1, dev(dz=k)) for k in (4, 3, 5, 2, 6, 1, 7)]

    for copy in c1:
        copy.wait_recv()
    for i in range(NX):
        total = s_c1[z, i].astype(F32)
        for k in range(NZ - 1):
            total += r_c1[k, i].astype(F32)
        s_c2[i] = total.astype(BF16)
    c2 = [push(s_c2.at[lax.rem(x + k, NX)], r_c2.at[k - 1], C2 + k - 1, dev(dx=k)) for k in (2, 1, 3)]

    for copy in a1:
        copy.wait_recv()

    def add_a(i, carry):
        total = s_a1[x, i].astype(F32)
        for k in range(NX - 1):
            total += r_a1[k, i].astype(F32)
        s_a2[i] = total.astype(BF16)
        return carry

    lax.fori_loop(0, NZ, add_a, 0)
    a2 = [push(s_a2.at[lax.rem(z + k, NZ)], r_a2.at[k - 1], A2 + k - 1, dev(dz=k)) for k in (4, 3, 5, 2, 6, 1, 7)]

    for copy in c2:
        copy.wait_recv()
    total = s_c2[x].astype(F32)
    for k in range(NX - 1):
        total += r_c2[k].astype(F32)
    sum3[2] = total
    for copy in a2:
        copy.wait_recv()
    total = s_a2[z].astype(F32)
    for k in range(NZ - 1):
        total += r_a2[k].astype(F32)
    sum3[0] = total[:, :LANE]
    sum3[1] = total[:, LANE:]

    pack_s[...] = jnp.zeros_like(pack_s)
    pack_o[...] = jnp.zeros_like(pack_o)
    for j in range(NY):
        for t in range(3):
            for r in range(2):
                pack_s[j, pl.ds(3 * r + t, 1), :] = sum3[t, pl.ds(3 * j + r + core, 1), :]
            pack_o[j, pl.ds(t, 1), :] = sum3[t, pl.ds(3 * j + 2 - 2 * core, 1), :]
    s_s[...] = pack_s[...].astype(BF16)
    s_o[...] = pack_o[...].astype(BF16)
    st = []
    for k in (4, 3, 5, 2, 6, 1, 7):
        to = lax.rem(y + k, NY)
        st.append(push(s_s.at[to], r_s.at[k - 1], SS + k - 1, dev(dy=k)))
        st.append(push(s_o.at[to], r_o.at[k], SO + k, dev(dy=k, flip=True)))
    st.append(push(s_o.at[y], r_o.at[0], SO, dev(flip=True)))
    for copy in st:
        copy.wait_recv()
    same = s_s[y].astype(F32)
    for k in range(NY - 1):
        same += r_s[k].astype(F32)
    rest = r_o[0].astype(F32)
    for k in range(1, NY):
        rest += r_o[k].astype(F32)
    flat[pl.ds(0, 3), :] = same[0:3]
    flat[pl.ds(3, 3), :] = rest[0:3]
    flat[pl.ds(6, 3), :] = same[3:6]

    gradient = flat[pl.ds(0, 9), :]
    moment_new = 0.9 * moment[...] + 0.1 * gradient
    second_new = 0.95 * second[...] + 0.05 * gradient * gradient
    first_fix = 1.0 - 0.9**STEP
    second_fix = 1.0 - 0.95**STEP
    ratio = moment_new / first_fix / (jnp.sqrt(second_new / second_fix) + 1e-08)
    master_new = master[...] - 0.01 * (ratio + 0.01 * master[...])
    master_out[...] = master_new
    moment_out[...] = moment_new
    second_out[...] = second_new

    pack_s[0, pl.ds(0, 3), :] = master_new[0:3]
    pack_s[0, pl.ds(3, 3), :] = master_new[6:9]
    pack_o[0, pl.ds(0, 3), :] = master_new[3:6]
    w3s[y] = pack_s[0].astype(BF16)
    s_wo[...] = pack_o[0].astype(BF16)
    wt = []
    for k in (4, 3, 5, 2, 6, 1, 7):
        wt.append(push(w3s.at[y], w3s.at[y], WS + k - 1, dev(dy=k)))
        wt.append(push(s_wo, w3o.at[y], WO + k, dev(dy=k, flip=True)))
    wt.append(push(s_wo, w3o.at[y], WO, dev(flip=True)))
    for copy in wt:
        copy.wait_recv()
    pack_s[...] = w3s[...].astype(F32)
    pack_o[...] = w3o[...].astype(F32)
    for j in range(NY):
        for t in range(3):
            for r in range(2):
                w24[t, pl.ds(3 * j + r + core, 1), :] = pack_s[j, pl.ds(3 * r + t, 1), :]
            w24[t, pl.ds(3 * j + 2 - 2 * core, 1), :] = pack_o[j, pl.ds(t, 1), :]
    for t in range(3):
        out[z, x, :, pl.ds(pl.multiple_of(core * HALF + t * LANE, LANE), LANE)] = w24[t].astype(BF16)

    al = pl.ds(pl.multiple_of(core * HALF, LANE), AW)
    cl = pl.ds(pl.multiple_of(core * HALF + AW, LANE), CW)
    block_a = out.at[z, x, :, al]
    block_c = out.at[z, x, :, cl]
    gc1 = [push(block_c, block_c, GC1 + k - 1, dev(dx=k)) for k in (2, 1, 3)]
    ga1 = [push(block_a, block_a, GA1 + k - 1, dev(dz=k)) for k in (4, 3, 5, 2, 6, 1, 7)]
    for copy in gc1:
        copy.wait_recv()
    slab_c = out.at[z, :, :, cl]
    gc2 = [push(slab_c, slab_c, GC2 + k - 1, dev(dz=k)) for k in (4, 3, 5, 2, 6, 1, 7)]
    for copy in ga1:
        copy.wait_recv()
    slab_a = out.at[:, x, :, al]
    ga2 = [push(slab_a, slab_a, GA2 + k - 1, dev(dx=k)) for k in (2, 1, 3)]

    dd = [push(slab_a, slab_a, DD, dev(flip=True)), push(slab_c, slab_c, DD + 1, dev(flip=True))]
    for n, k in enumerate((7, 1, 6, 2, 5, 3, 4)):
        gc2[6 - n].wait_recv()
        slab = out.at[lax.rem(z + NZ - k, NZ), :, :, cl]
        dd.append(push(slab, slab, DD + 2 + n, dev(flip=True)))
    for n, k in enumerate((3, 1, 2)):
        ga2[2 - n].wait_recv()
        slab = out.at[:, lax.rem(x + NX - k, NX), :, al]
        dd.append(push(slab, slab, DD + 9 + n, dev(flip=True)))
    for copy in dd:
        copy.wait_recv()
    for copy in sends:
        copy.wait_send()


def shards(acts, grads_out, master, moment, second):
    vmem = pl.BlockSpec(memory_space=pltpu.VMEM)
    anyw = pl.BlockSpec(memory_space=pl.ANY)
    small = jax.ShapeDtypeStruct(master.shape, F32)
    tokens, width = acts.shape
    master_new, moment_new, second_new, out = pl.pallas_call(
        kernel,
        out_shape=(small, small, small, jax.ShapeDtypeStruct((NZ, NX, ROWS, 2 * HALF), BF16)),
        in_specs=[anyw, anyw, vmem, vmem, vmem],
        out_specs=(vmem, vmem, vmem, vmem),
        scratch_shapes=[
            pltpu.VMEM((tokens, width), BF16),
            pltpu.VMEM((tokens, width), BF16),
            pltpu.VMEM((width, width), F32),
            pltpu.VMEM((NZ * NX, ROWS, HALF), BF16),
            pltpu.VMEM((NZ * NX, ROWS, HALF), BF16),
            pltpu.VMEM((NX, NZ, ROWS, AW), BF16),
            pltpu.VMEM((NX - 1, NZ, ROWS, AW), BF16),
            pltpu.VMEM((NZ, NX, ROWS, CW), BF16),
            pltpu.VMEM((NZ - 1, NX, ROWS, CW), BF16),
            pltpu.VMEM((NZ, ROWS, AW), BF16),
            pltpu.VMEM((NZ - 1, ROWS, AW), BF16),
            pltpu.VMEM((NX, ROWS, CW), BF16),
            pltpu.VMEM((NX - 1, ROWS, CW), BF16),
            pltpu.VMEM((3, ROWS, LANE), F32),
            pltpu.VMEM((NY, 8, LANE), F32),
            pltpu.VMEM((NY, 8, LANE), F32),
            pltpu.VMEM((NY, 8, LANE), BF16),
            pltpu.VMEM((NY, 8, LANE), BF16),
            pltpu.VMEM((NY - 1, 8, LANE), BF16),
            pltpu.VMEM((NY, 8, LANE), BF16),
            pltpu.VMEM((16, LANE), F32),
            pltpu.VMEM((NY, 8, LANE), BF16),
            pltpu.VMEM((NY, 8, LANE), BF16),
            pltpu.VMEM((8, LANE), BF16),
            pltpu.VMEM((3, ROWS, LANE), F32),
            pltpu.SemaphoreType.DMA((NSEM,)),
            pltpu.SemaphoreType.DMA((NSEM,)),
            pltpu.SemaphoreType.DMA((3,)),
        ],
        compiler_params=pltpu.CompilerParams(collective_id=0, has_side_effects=True),
        name="step",
    )(acts, grads_out, master, moment, second)
    return master_new, moment_new, second_new, out.reshape(width, width)


def solution(mesh):
    spec = P(("gx", "gy", "gz"), None)
    return jax.shard_map(
        shards, mesh=mesh, in_specs=(spec,) * 5, out_specs=(spec, spec, spec, P()), check_vma=False)
```

time: 133 us -> 63.1 us (0.47)
  blocking collectives: 119 us -> 0 us
  Pallas kernels: 0 us -> 55.8 us
  matrix products: 4.3 us -> 0 us
  other arithmetic: 2.12 us -> 0 us
    all_to_all x6 -> x0, blocking collectives: 119 us -> none  [the longest x3 68.2 us: sent_and_summed(): lax.all_to_all(parts, axis, split_axis=0, concat_axis=0, tiled=True)]
    pallas_call x0 -> x1, Pallas kernels: none -> 55.8 us  [shards(): pl.pallas_call(kernel, out_shape=(small, small, small, jax.ShapeDtypeStru...]
    unnamed x8 -> x4, local copies, waits for them, and re-layouts: 1.56 us -> 6.24 us
    dot_general x1 -> x0, matrix products: 4.3 us -> none  [shards(): lax.dot_general(acts, grads_out, (((0,), (0,)), ((), ())), preferred_elem...]
    convert_element_type x1 -> x0, local copies, waits for them, and re-layouts: 2.56 us -> none  [shards(): partial_value = sent_and_summed(local_flat.astype(jnp.bfloat16), 'gx', 0)]
    another operation x1 -> x0, local copies, waits for them, and re-layouts: 1.85 us -> none  [shards(): weights = gathered.reshape(width_in, width_out)]
    reduce_sum x3 -> x0, other arithmetic: 1.49 us -> none  [sent_and_summed(): return arrived.astype(jnp.float32).sum(axis=0)]
where the time goes in v1:
time: 63.1 us; the launch traced here: 62.7 us
  Pallas kernels  55.8 us (88%)
  local copies, waits for them, and re-layouts  6.24 us (10%)
  between operations  0.64 us (1%)
    pallas_call x1, Pallas kernels, shards(): pl.pallas_call(kernel, out_shape=(small, small, small, jax.ShapeDtypeStru...  55.8 us
    unnamed x4, local copies, waits for them, and re-layouts  6.24 us

profile of v1, /device:TPU:1, one launch (start us, length us, event | category | flops | bytes accessed | tf_op | source)
XLA Modules:
  0.0 62.7 jit_solution(15331932577331232869)
XLA Ops:
  0.6 55.8 %step.1 = (f32[9,128]{1,0:T(8,128)}, f32[9,128]{1,0:T(8,128)}, f32[9,128]{1,0:T(8,128)}, bf16[8,4,24,768]{3,2,1,0:T(8,128)(2,1)}) custom-call(bf16[1280,768]{1,0:T(8,128)(2,1)} %acts.1, bf16[1280,768]{1,0:T(8,128)(2,1)} %grads.1, f32[9,128]{1,0:T(8,128)} %master.1, f32[9,128]{1,0:T(8,128)} %moment.1, f32[9,128]{1,0:T(8,128)} %second.1), custom_call_target="tpu_custom_call" | custom-call | tf_op jit(solution)/shard_map/step/pallas_call | solution.py:233
  56.4 1.3 %copy.13 = f32[9,128]{1,0:T(8,128)} copy(f32[9,128]{1,0:T(8,128)} %get-tuple-element.16) | data formatting | bytes 9216
  57.7 1.3 %copy.14 = f32[9,128]{1,0:T(8,128)} copy(f32[9,128]{1,0:T(8,128)} %get-tuple-element.17) | data formatting | bytes 9216
  59.0 1.3 %copy.15 = f32[9,128]{1,0:T(8,128)} copy(f32[9,128]{1,0:T(8,128)} %get-tuple-element.18) | data formatting | bytes 9216
  60.3 2.4 %copy.16 = bf16[768,768]{1,0:T(8,128)(2,1)} copy(bf16[768,768]{1,0:T(8,128)(2,1)} %bitcast.1) | data formatting | bytes 2359296
